TPU v7x, 16 devices: a whole 2x2x2 slice. The times are simulated.
16 devices in a mesh: dp: 2 (over z), tp: 8 (over y, x, core).
Axes of the slice: x: 2, y: 2, z: 2, core: 2. Of those that a mesh axis runs over, the one named last changes fastest.
Arguments:
- token_ids: int32 [16384], P('dp'), parts along dimension 0
- positions: int32 [16384], P('dp'), parts along dimension 0
- embed_table: bfloat16 [256000, 2304], P('tp')
- norm_scale: float32 [2304], replicated
- w_query: bfloat16 [2304, 2048], P(None, 'tp')
- w_key: bfloat16 [2304, 1024], replicated
- w_value: bfloat16 [2304, 1024], replicated
Outputs:
- output 1: bfloat16 [16384, 2304], P(('dp', 'tp')), parts along dimension 0
- output 2: bfloat16 [16384, 8, 256], P('dp', 'tp'), parts along dimension 0
- output 3: bfloat16 [16384, 8, 256], P('dp', 'tp'), parts along dimension 0
- output 4: bfloat16 [16384, 8, 256], P('dp', 'tp'), parts along dimension 0
There are 2 independent parts. A program takes and returns all parts, laid end to end along the dimension named above; an argument that names none is the same for every part.
All inputs are finite; a program needn't handle non-finite values.
Results may differ from a plain program's by a relative error of at most 0.0120345.
Values are sent between devices in bfloat16 or wider.
A program may use at most 1 GiB of HBM per device.

v0:
```python
import functools
import math
import jax
import jax.numpy as jnp
from jax import lax
from jax.experimental import pallas as pl
from jax.experimental.pallas import tpu as pltpu
from jax.sharding import PartitionSpec as P

HEAD_DIM = 256
EPSILON = 1e-6
ROPE_BASE = 10000.0
TILE = 128
SLOTS = 6
CHUNKS = 2
HEAD_ROWS = 640
TAIL_ROWS = 640
SEND_ROWS = 512
CHIPS = 4
MESH_IDS = pl.DeviceIdType.MESH


def rope_tables(positions):
    inv_freq = ROPE_BASE ** (-jnp.arange(0, HEAD_DIM, 2, dtype=jnp.float32) / HEAD_DIM)
    angles = positions.astype(jnp.float32)[:, None] * inv_freq[None, :]
    return jnp.cos(angles), jnp.sin(angles)


def gather_kernel(base, tiles, width, pair_ids, counts, cols_ref, table_ref, *rest):
    out_ref, pairs, sems = rest[-3:]
    step = pl.program_id(0)
    normalizer = jnp.asarray(math.sqrt(width), dtype=jnp.bfloat16)

    def start(tile, slot):
        count = counts[base + tile]

        def copy(group, row):
            src = pair_ids[(base + tile) * TILE + group * 8 + row]
            pltpu.make_async_copy(table_ref.at[pl.ds(pl.multiple_of(src, 2), 2), :], pairs.at[slot, group, pl.ds(2 * row, 2), :], sems.at[slot]).start()

        @pl.loop(0, count // 8)
        def _(group):
            for row in range(8):
                copy(group, row)

        for row in range(7):
            @pl.when(row < lax.rem(count, 8))
            def _():
                copy(count // 8, row)

    def wait(tile, slot):
        count = counts[base + tile]
        size = TILE // 8
        while size:
            @pl.when((count // (8 * size)) % 2 == 1)
            def _():
                pltpu.make_async_copy(pairs.at[slot, pl.ds(0, size)], pairs.at[slot, pl.ds(0, size)], sems.at[slot]).wait()

            size //= 2
        for size in (1, 2, 4):
            @pl.when((count // size) % 2 == 1)
            def _():
                pltpu.make_async_copy(table_ref.at[pl.ds(0, 2 * size), :], pairs.at[slot, 0, pl.ds(0, 2 * size), :], sems.at[slot]).wait()

    @pl.when(step == 0)
    def _():
        pairs[...] = jnp.zeros_like(pairs)

        @pl.loop(0, min(SLOTS - 1, tiles))
        def _(tile):
            start(tile, tile)

    slot = lax.rem(step, SLOTS)

    @pl.when(step + SLOTS - 1 < tiles)
    def _():
        start(step + SLOTS - 1, lax.rem(step + SLOTS - 1, SLOTS))

    wait(step, slot)
    lanes = lax.broadcasted_iota(jnp.int32, (TILE, 2 * TILE), 1).astype(jnp.float32)
    wanted = jnp.broadcast_to(cols_ref[base + step], (TILE, TILE)).T
    select = jnp.where(lanes == jnp.concatenate([wanted, wanted], axis=1), normalizer, jnp.zeros((), jnp.bfloat16))
    for piece in range(width // 256):
        cols = pl.ds(piece * 256, 256)
        picked = jnp.dot(select, pairs[slot, :, :, cols].reshape(2 * TILE, 256), preferred_element_type=jnp.float32)
        out_ref[:, cols] = picked.astype(jnp.bfloat16)


def gather_rows(base, count, pair_ids, counts, cols, table_rows, after):
    width = table_rows.shape[1]
    tiles = count // TILE
    base = base // TILE
    anywhere = pl.BlockSpec(memory_space=pl.ANY)
    grid_spec = pltpu.PrefetchScalarGridSpec(
        num_scalar_prefetch=2,
        grid=(tiles,),
        in_specs=[pl.BlockSpec(cols.shape, lambda i, *_: (0, 0, 0)), anywhere] + [anywhere] * len(after),
        out_specs=pl.BlockSpec((TILE, width), lambda i, *_: (i, 0)),
        scratch_shapes=[pltpu.VMEM((SLOTS, TILE // 8, 16, width), jnp.bfloat16), pltpu.SemaphoreType.DMA((SLOTS,))],
    )
    return pl.pallas_call(
        functools.partial(gather_kernel, base, tiles, width),
        grid_spec=grid_spec,
        out_shape=jax.ShapeDtypeStruct((count, width), jnp.bfloat16),
        compiler_params=pltpu.CompilerParams(dimension_semantics=("arbitrary",)),
        cost_estimate=pl.CostEstimate(flops=count * 20_000_000, bytes_accessed=count * width * 6, transcendentals=0),
        name="gather_rows",
    )(pair_ids, counts, cols, table_rows, *after)


def rows_kernel(pieces, head_rows, first_place, last, more, cols_ref, gain_ref, base_hbm, extra_hbm, *refs):
    piece_refs, refs = refs[:pieces], refs[pieces:]
    if last:
        resid_hbm, normed_hbm, source, parts, extra, resid, normed, in_sems, out_sems = refs
    else:
        resid_hbm, source, parts, resid, in_sems, out_sems = refs
    rows, width = resid.shape
    known = source.shape[0]
    part = parts.shape[2]
    one = jnp.ones((), jnp.bfloat16)
    zero = jnp.zeros((), jnp.bfloat16)
    copies = [pltpu.make_async_copy(base_hbm, resid if last else source.at[pl.ds(0, head_rows), :], in_sems.at[pieces])]
    for index, ref in enumerate(piece_refs):
        there = source.at[pl.ds(head_rows + index // 3 * part, part), :] if index % 3 == 0 else parts.at[index // 3, index % 3 - 1]
        copies.append(pltpu.make_async_copy(ref.at[pl.ds(0, part), :], there, in_sems.at[index]))
    for copy in copies:
        copy.start()
    for copy in copies:
        copy.wait()
    for index in range(pieces // 3):
        span = pl.ds(head_rows + index * part, part)
        source[span, :] = source[span, :] + parts[index, 0] + parts[index, 1]
    if last:
        @pl.when(more[0] > 0)
        def _():
            extra_copy = pltpu.make_async_copy(extra_hbm, extra, in_sems.at[pieces + 1])
            extra_copy.start()
            extra_copy.wait()

    def results(block):
        span = pl.ds(pl.multiple_of(block * 256, 256), 256)
        copies = [pltpu.make_async_copy(resid.at[span, :], resid_hbm.at[span, :], out_sems.at[0])]
        if last:
            copies.append(pltpu.make_async_copy(normed.at[span, :], normed_hbm.at[span, :], out_sems.at[1]))
        return copies

    @pl.loop(0, rows // 256)
    def _(block):
        span = pl.ds(pl.multiple_of(block * 256, 256), 256)

        def add(values, first):
            count = values.shape[0]
            places = lax.broadcasted_iota(jnp.int32, (256, count), 1) + first
            select = jnp.where(places == cols_ref[span, :], one, zero)
            for piece in range(width // 256):
                cols = pl.ds(piece * 256, 256)
                picked = jnp.dot(select, values[:, cols], preferred_element_type=jnp.float32)
                resid[span, cols] = (resid[span, cols].astype(jnp.float32) + picked).astype(jnp.bfloat16)

        if last:
            add(source, first_place)

            @pl.when(more[0] > 0)
            def _():
                add(extra, first_place + known)

            for quarter in range(4):
                rows_here = pl.ds(pl.multiple_of(block * 256 + quarter * 64, 64), 64)
                widened = resid[rows_here, :].astype(jnp.float32)
                inv_rms = lax.rsqrt(jnp.mean(widened * widened, axis=-1, keepdims=True) + EPSILON)
                normed[rows_here, :] = (widened * inv_rms * gain_ref[...]).astype(jnp.bfloat16)
        else:
            normalizer = jnp.asarray(math.sqrt(width), dtype=jnp.bfloat16)
            lanes = lax.broadcasted_iota(jnp.int32, (256, known), 1)
            value = jnp.where(lax.broadcasted_iota(jnp.int32, (1, known), 1) < head_rows, normalizer, one)
            select = jnp.where(lanes == cols_ref[span, :], jnp.broadcast_to(value, (256, known)), zero)
            for piece in range(width // 256):
                cols = pl.ds(piece * 256, 256)
                resid[span, cols] = jnp.dot(select, source[:, cols], preferred_element_type=jnp.float32).astype(jnp.bfloat16)
        for result in results(block):
            result.start()

    @pl.loop(0, rows // 256)
    def _(block):
        for result in results(block):
            result.wait()


def pick_rows(first_place, last, more, cols, gain, base, extra, pieces):
    rows = cols.shape[0]
    width = base.shape[1]
    head_rows = 0 if last else base.shape[0]
    part = pieces[0].shape[0]
    known = head_rows + part * len(pieces) // 3
    vmem = pl.BlockSpec(memory_space=pltpu.VMEM)
    anywhere = pl.BlockSpec(memory_space=pl.ANY)
    shape = jax.ShapeDtypeStruct((rows, width), jnp.bfloat16)
    dma = pltpu.SemaphoreType.DMA
    block = pltpu.VMEM((rows, width), jnp.bfloat16)
    scratch = [pltpu.VMEM((known, width), jnp.bfloat16), pltpu.VMEM((len(pieces) // 3, 2, part, width), jnp.bfloat16)]
    scratch += [pltpu.VMEM(extra.shape, jnp.bfloat16), block, block] if last else [block]
    return pl.pallas_call(
        functools.partial(rows_kernel, len(pieces), head_rows, first_place, last),
        out_shape=(shape, shape) if last else shape,
        in_specs=[pl.BlockSpec(memory_space=pltpu.SMEM), vmem, vmem, anywhere, anywhere] + [anywhere] * len(pieces),
        out_specs=(anywhere, anywhere) if last else anywhere,
        scratch_shapes=scratch + [dma((len(pieces) + 2,)), dma((2,))],
        compiler_params=pltpu.CompilerParams(vmem_limit_bytes=67_043_328),
        cost_estimate=pl.CostEstimate(flops=2 * rows * width * known, bytes_accessed=16_000_000, transcendentals=0),
        name="pick_rows",
    )(more, cols, gain, base, extra, *pieces)


def heads_kernel(rows, normed_hbm, cos_ref, sin_ref, wq_mine, wq_far, wq_near, wk_hbm, wv_hbm, q_out, kv_out,
                 wq, wk, wv, normed, q_stage, kv_stage, w_sem, q_send, q_recv, kv_send, kv_recv,
                 own_recv, fwd_send, fwd_recv, keep_sem):
    group = lax.axis_index("dp")
    me = lax.axis_index("tp")
    core = lax.rem(me, 2)
    chip = me // 2
    partner = me + 1 - 2 * core
    kv_outs = (kv_out.at[0], kv_out.at[1])
    tiles = rows // SEND_ROWS
    half = HEAD_DIM // 2

    depth = wq_mine.shape[1]
    own_depth = pl.ds(pl.multiple_of(group * depth, depth), depth)
    far_depth = pl.ds(pl.multiple_of((1 - group) * depth, depth), depth)
    sources = ((normed_hbm, normed), (wk_hbm, wk), (wv_hbm, wv), (wq_mine, wq.at[:, own_depth, :]),
               (wq_far, wq.at[pl.ds(core * CHIPS, CHIPS), far_depth, :]), (wq_near, wq.at[pl.ds((1 - core) * CHIPS, CHIPS), far_depth, :]))
    loads = [pltpu.make_async_copy(src, dst, w_sem.at[n]) for n, (src, dst) in enumerate(sources)]
    for load in loads[:2]:
        load.start()

    barrier = pltpu.get_barrier_semaphore()
    for step in range(1, 2 * CHIPS):
        pl.semaphore_signal(barrier, inc=1, device_id=(group, lax.rem(me + step, 2 * CHIPS)), device_id_type=MESH_IDS)

    pl.semaphore_wait(barrier, 2 * CHIPS - 1)
    for load in loads[:2]:
        load.wait()
    for load in loads[2:]:
        load.start()

    def block(source, tile):
        return pl.ds(pl.multiple_of(source * rows + tile * SEND_ROWS, SEND_ROWS), SEND_ROWS)

    def whole(source):
        return pl.ds(pl.multiple_of(source * rows, rows), rows)

    def remote(src, dst, send, recv, device):
        return pltpu.make_async_remote_copy(src_ref=src, dst_ref=dst, send_sem=send, recv_sem=recv, device_id=(group, device), device_id_type=MESH_IDS)

    def rotated(linear, span, factor):
        front = linear[:, :half]
        back = linear[:, half:]
        cosines = cos_ref[span, :]
        sines = sin_ref[span, :]
        return jnp.concatenate([((front * cosines - back * sines) * factor).astype(jnp.bfloat16), ((back * cosines + front * sines) * factor).astype(jnp.bfloat16)], axis=-1)

    @pl.loop(0, CHIPS * tiles)
    def _(turn):
        offset = lax.rem(turn // tiles + 1, CHIPS)
        tile = lax.rem(turn, tiles)
        there = lax.rem(chip + offset, CHIPS)
        columns = pl.ds(pl.multiple_of(there * HEAD_DIM, HEAD_DIM), HEAD_DIM)
        sent = pl.ds(pl.multiple_of(tile * SEND_ROWS, SEND_ROWS), SEND_ROWS)

        @pl.loop(0, SEND_ROWS // 256)
        def _(part):
            span = pl.ds(pl.multiple_of(tile * SEND_ROWS + part * 256, 256), 256)
            lhs = normed[span, :]

            def linear(weight):
                return jnp.dot(lhs, weight, preferred_element_type=jnp.float32).astype(jnp.bfloat16)

            def arrived(weights):
                @pl.when(turn + part == 0)
                def _():
                    for load in weights:
                        load.wait()

            kv_stage[0, there, span, :] = rotated(linear(wk[:, columns]).astype(jnp.float32), span, 1.0)
            arrived(loads[2:3])
            kv_stage[1, there, span, :] = linear(wv[:, columns])
            arrived(loads[3:])
            for side in range(2):
                q_stage[2 * there + side, span, :] = rotated(linear(wq[2 * there + side]).astype(jnp.float32), span, HEAD_DIM ** -0.5)

        @pl.when(offset != 0)
        def _():
            for side in range(2):
                remote(kv_stage.at[side, there, sent, :], kv_outs[side].at[block(me, tile), :], kv_send.at[offset, side], kv_recv.at[offset, core, tile], 2 * there + side).start()
            for side in range(2):
                remote(q_stage.at[2 * there + side, sent, :], q_out.at[block(me, tile), :], q_send.at[offset, side], q_recv.at[offset, core], 2 * there + side).start()

    for side in range(2):
        remote(kv_stage.at[side, chip], kv_outs[side].at[whole(me), :], kv_send.at[0, side], own_recv.at[side], partner).start()
    remote(q_stage.at[partner], q_out.at[whole(me), :], q_send.at[0, 0], q_recv.at[0, 0], partner).start()
    keeps = [pltpu.make_async_copy(q_stage.at[me], q_out.at[whole(me), :], keep_sem.at[0])]
    for side in range(2):
        keeps.append(pltpu.make_async_copy(kv_stage.at[side, chip], kv_outs[side].at[whole(me), :], keep_sem.at[1 + side]))
    for keep in keeps:
        keep.start()

    def forward(mine_out, other_out):
        for tile in range(tiles):
            for offset in range(1, CHIPS):
                for side in range(2):
                    source = 2 * lax.rem(chip + CHIPS - offset, CHIPS) + side
                    region = mine_out.at[block(source, tile), :]
                    remote(region, region, kv_send.at[offset, side], kv_recv.at[offset, side, tile], partner).wait_recv()
                    remote(region, region, fwd_send.at[offset, side], fwd_recv.at[offset, side], partner).start()
        for offset in range(1, CHIPS):
            for side in range(2):
                source = 2 * lax.rem(chip + CHIPS - offset, CHIPS) + side
                mine = mine_out.at[whole(source), :]
                remote(mine, mine, fwd_send.at[offset, side], fwd_recv.at[offset, side], partner).wait_send()
                other = other_out.at[whole(source), :]
                remote(other, other, fwd_send.at[offset, side], fwd_recv.at[offset, side], partner).wait_recv()

    forward(kv_out.at[core], kv_out.at[1 - core])

    for keep in keeps:
        keep.wait()
    for offset in range(1, CHIPS):
        there = lax.rem(chip + offset, CHIPS)
        for side in range(2):
            source = 2 * lax.rem(chip + CHIPS - offset, CHIPS) + side
            remote(kv_stage.at[side, there], kv_outs[side].at[whole(me), :], kv_send.at[offset, side], own_recv.at[side], partner).wait_send()
            remote(q_stage.at[2 * there + side], q_out.at[whole(source), :], q_send.at[offset, side], q_recv.at[offset, side], partner).wait()
    for side in range(2):
        remote(kv_stage.at[side, chip], kv_outs[side].at[whole(partner), :], kv_send.at[0, side], own_recv.at[side], partner).wait()
    remote(q_stage.at[partner], q_out.at[whole(partner), :], q_send.at[0, 0], q_recv.at[0, 0], partner).wait()


def project_heads(normed, cosines, sines, wq_parts, w_key, w_value):
    rows, width = normed.shape
    heads = wq_parts[0].shape[0]
    tokens = rows * heads
    tiles = rows // SEND_ROWS
    vmem = pl.BlockSpec(memory_space=pltpu.VMEM)
    anywhere = pl.BlockSpec(memory_space=pl.ANY)
    dma = pltpu.SemaphoreType.DMA
    return pl.pallas_call(
        functools.partial(heads_kernel, rows),
        out_shape=(jax.ShapeDtypeStruct((tokens, HEAD_DIM), jnp.bfloat16), jax.ShapeDtypeStruct((2, tokens, HEAD_DIM), jnp.bfloat16)),
        in_specs=[anywhere, vmem, vmem] + [anywhere] * 5,
        out_specs=(anywhere, anywhere),
        scratch_shapes=[
            pltpu.VMEM((heads, width, HEAD_DIM), jnp.bfloat16),
            pltpu.VMEM(w_key.shape, jnp.bfloat16),
            pltpu.VMEM(w_value.shape, jnp.bfloat16),
            pltpu.VMEM((rows, width), jnp.bfloat16),
            pltpu.VMEM((heads, rows, HEAD_DIM), jnp.bfloat16),
            pltpu.VMEM((2, CHIPS, rows, HEAD_DIM), jnp.bfloat16),
            dma((6,)),
            dma((CHIPS, 2)), dma((CHIPS, 2)),
            dma((CHIPS, 2)), dma((CHIPS, 2, tiles)),
            dma((2,)),
            dma((CHIPS, 2)), dma((CHIPS, 2)),
            dma((3,)),
        ],
        compiler_params=pltpu.CompilerParams(collective_id=0, has_side_effects=True, vmem_limit_bytes=67_043_328),
        cost_estimate=pl.CostEstimate(flops=2 * rows * width * 4096, bytes_accessed=40_000_000, transcendentals=0),
        name="project_heads",
    )(normed, cosines, sines, *wq_parts, w_key, w_value)


def solution(mesh):
    group_size = mesh.shape["tp"]

    def exchange(rows, bit):
        return lax.ppermute(rows, "tp", [(i, i ^ bit) for i in range(group_size)])

    def pass_head(values, pairs, after=None):
        got = lax.ppermute(values, "tp", pairs)
        if after is not None:
            got, _ = lax.optimization_barrier((got, after))
        return jnp.where(lax.axis_index("tp") == pairs[0][1], got, values)

    def share_head(rows):
        half = rows.shape[0] // 2
        first = pass_head(rows[:half], [(0, 2)])
        second = pass_head(rows[half:], [(0, 4)])
        first = pass_head(first, [(2, 6)])
        second = pass_head(second, [(4, 6)])
        return first, second

    def share_head_back(first, second, after):
        first = pass_head(first, [(6, 4)], after)
        second = pass_head(second, [(6, 2)], after)
        both = jnp.concatenate([first, second], axis=0)
        other = lax.ppermute(both, "tp", [(0, 1), (2, 3), (4, 5), (6, 7)])
        return jnp.where(lax.axis_index("tp") % 2 == 1, other, both)

    def local_body(token_ids, positions, table_rows, norm_scale, w_query, w_key, w_value):
        dev_index = lax.axis_index("tp")
        vocab_rows, model_width = table_rows.shape
        group = lax.axis_index("dp")
        core = dev_index % 2
        part_rows = w_query.shape[0] // 2
        wq_mine = lax.all_gather(lax.dynamic_slice_in_dim(w_query, group * part_rows, part_rows, axis=0), "tp", axis=0)
        wq_far = lax.ppermute(lax.dynamic_slice_in_dim(wq_mine, core * (group_size // 2), group_size // 2, axis=0), "dp", [(0, 1), (1, 0)])
        wq_near = exchange(wq_far, 1)
        head_halves = share_head(table_rows[:HEAD_ROWS])
        tokens = token_ids.shape[0]
        block_rows = tokens // group_size
        extra_rows = block_rows - TAIL_ROWS
        chunk_rows = TAIL_ROWS // CHUNKS
        half = chunk_rows // 2

        blocks = token_ids.reshape(group_size, block_rows)
        in_tail = blocks >= HEAD_ROWS
        earlier = (lax.broadcasted_iota(jnp.int32, (block_rows, block_rows), 0) < lax.broadcasted_iota(jnp.int32, (block_rows, block_rows), 1)).astype(jnp.bfloat16)
        ranks = jnp.dot(in_tail.astype(jnp.bfloat16), earlier, preferred_element_type=jnp.float32).astype(jnp.int32)
        ranks = jnp.where(in_tail, ranks, -1)

        def ranked_ids(first, count):
            wanted = lax.broadcasted_iota(jnp.int32, (group_size, block_rows, count), 2) + first
            ids = jnp.sum(jnp.where(ranks[:, :, None] == wanted, blocks[:, :, None] + 1, 0), axis=1) - 1
            local = ids - dev_index * vocab_rows
            return jnp.where((ids >= 0) & (local >= 0) & (local < vocab_rows), local, -1)

        most = jnp.max(jnp.sum(in_tail.astype(jnp.int32), axis=1))
        over = (most > TAIL_ROWS).astype(jnp.int32)

        def arrange(values):
            view = values.reshape(2, 2, 2, CHUNKS, 2, half)
            for axis, bit in ((0, 4), (1, 2), (2, 1)):
                flag = (dev_index // bit) % 2 == 1
                view = jnp.where(flag, jnp.flip(view, axis), view)
            halves = view.transpose(3, 2, 4, 0, 1, 5)
            first = halves[:, :, 0].transpose(0, 1, 3, 2, 4)
            second = halves[:, :, 1]
            return jnp.stack([first, second], axis=2).reshape(CHUNKS, 2, 4 * chunk_rows)

        call_rows = 4 * chunk_rows
        ids = arrange(ranked_ids(0, TAIL_ROWS)).reshape(-1, TILE)
        owned = ids >= 0
        before = (lax.broadcasted_iota(jnp.int32, (TILE, TILE), 0) < lax.broadcasted_iota(jnp.int32, (TILE, TILE), 1)).astype(jnp.bfloat16)
        slots = jnp.dot(owned.astype(jnp.bfloat16), before, preferred_element_type=jnp.float32).astype(jnp.int32)
        slots = jnp.where(owned, slots, -1)
        wanted_slot = lax.broadcasted_iota(jnp.int32, (ids.shape[0], TILE, TILE), 2)
        pair_ids = jnp.sum(jnp.where(slots[:, :, None] == wanted_slot, (ids // 2)[:, :, None] * 2, 0), axis=1).reshape(-1)
        cols = jnp.where(owned, 2 * slots + ids % 2, -1).astype(jnp.float32)[:, None, :]
        counts = jnp.sum(owned.astype(jnp.int32), axis=-1)

        def gather(chunk, side, after):
            return gather_rows((2 * chunk + side) * call_rows, call_rows, pair_ids, counts, cols, table_rows, after)

        pieces, sums = [], []
        after, late, late_next = [], [], []
        for chunk in range(CHUNKS):
            other = gather(chunk, 1, after + late + ([wq_mine] if chunk == CHUNKS - 1 else []))
            got = exchange(other, 1)
            mine = gather(chunk, 0, [other])
            after, late = [], late_next
            late_next = []
            spans = []
            for part in range(2):
                first_row = part * 4 * half
                spans += [slice(first_row, first_row + half), slice(first_row + half, first_row + 2 * half), slice(first_row + 2 * half, first_row + 4 * half)]
            both = lax.optimization_barrier([mine[span] + got[span] for span in spans])
            for part, bits in ((0, (2, 4)), (1, (4, 2))):
                kept, near, sent = both[3 * part:3 * part + 3]
                back = exchange(sent, bits[0])
                near_send = near + back[half:]
                back2 = exchange(near_send, bits[1])
                after.append(sent)
                sums.append(near_send)
                late_next.append(near_send)
                pieces += [kept, back, back2]

        head = share_head_back(*head_halves, sums[1])

        def second_exchange(rows):
            ids = ranked_ids(TAIL_ROWS, extra_rows).reshape(-1)
            normalizer = jnp.asarray(math.sqrt(model_width), dtype=jnp.bfloat16)
            picked = jnp.take(rows, jnp.maximum(ids, 0), axis=0, mode="clip") * normalizer
            partial = jnp.where(ids[:, None] >= 0, picked, jnp.zeros((), jnp.bfloat16))
            return lax.psum_scatter(partial, "tp", scatter_dimension=0, tiled=True)

        def no_exchange(rows):
            return jnp.zeros((extra_rows, model_width), jnp.bfloat16)

        over, _ = lax.optimization_barrier((over, sums[1]))
        more = lax.pmax(over, "dp")
        extra = lax.cond(more > 0, second_exchange, no_exchange, table_rows)
        places = jnp.where(in_tail, HEAD_ROWS + ranks, blocks)
        own_places = lax.dynamic_index_in_dim(places, dev_index, 0, keepdims=False)
        asked, own_cols, gain = more.reshape(1), own_places[:, None], (1.0 + norm_scale)[None, :]
        split = len(pieces) // CHUNKS
        started = pick_rows(0, False, asked, own_cols, gain, head, extra, pieces[:split])
        residual, normed = pick_rows(HEAD_ROWS + TAIL_ROWS // CHUNKS, True, asked, own_cols, gain, started, extra, pieces[split:])
        own = lax.dynamic_slice_in_dim(positions, dev_index * block_rows, block_rows)
        cosines, sines = rope_tables(own)
        queries, keys_values = project_heads(normed, cosines, sines, (wq_mine, wq_far, wq_near), w_key, w_value)
        return residual, queries[:, None, :], keys_values[0][:, None, :], keys_values[1][:, None, :]

    head_spec = P("dp", "tp", None)
    return jax.shard_map(local_body, mesh=mesh, in_specs=(P("dp"), P("dp"), P("tp", None), P(), P(None, "tp"), P(), P()), out_specs=(P(("dp", "tp"), None), head_spec, head_spec, head_spec), check_vma=False)
```

profile of v0, /device:TPU:3, one launch (start us, length us, event | category | flops | bytes accessed | tf_op | source)
XLA Modules:
  0.0 364.2 jit_solution(3779388833220599823)
XLA Ops:
  7.2 3.1 fusion.13
  11.1 1.9 collective-permute-start.5
  13.0 1.9 constant_dynamic-slice_fusion.1
  16.6 3.0 select_reduce_fusion.1
  20.3 1.4 fusion.9
  21.6 2.6 select_reduce_fusion.2
  24.2 9.6 %gather_rows.4.rest_0_ = bf16[1280,2304]{1,0:T(8,128)(2,1)} custom-call(s32[5120]{0:T(1024)} %bitcast.38, s32[40]{0:T(128)} %get-tuple-element.81.counts, f32[40,1,128]{2,1,0:T(1,128)} %bitcast.42, bf16[32000,2304]{1,0:T(8,128)(2,1)} %table_ref.7), custom_call_target="tpu_custom_call" | custom-call | flops 25600000000 | bytes 17694720 | tf_op jit(solution)/shard_map/gather_rows/pallas_call | solution.py:101
  33.9 1.3 collective-permute-start
  35.2 1.1 copy-done.9
  36.3 2.1 broadcast_select_fusion.2
  38.4 1.8 collective-permute-start.6
  40.2 1.9 collective-permute-start.3
  42.0 9.7 %gather_rows.5 = bf16[1280,2304]{1,0:T(8,128)(2,1)} custom-call(s32[5120]{0:T(1024)} %bitcast.39, s32[40]{0:T(128)} %get-tuple-element.81.counts, f32[40,1,128]{2,1,0:T(1,128)} %bitcast.43, bf16[32000,2304]{1,0:T(8,128)(2,1)} %table_ref.7, bf16[1280,2304]{1,0:T(8,128)(2,1)} %gather_rows.4.rest_0_), custom_call_target="tpu_custom_call" | custom-call | flops 25600000000 | bytes 17694720 | tf_op jit(solution)/shard_map/gather_rows/pallas_call | solution.py:101
  51.8 1.3 broadcast_select_fusion.3
  53.0 1.9 collective-permute-start.7
  55.1 1.9 collective-permute-start.4
  57.0 3.6 slice_add_fusion.12
  60.6 3.4 slice_add_fusion.2
  65.1 9.6 %gather_rows.6.rest_0_ = bf16[1280,2304]{1,0:T(8,128)(2,1)} custom-call(s32[5120]{0:T(1024)} %bitcast.40, s32[40]{0:T(128)} %get-tuple-element.81.counts, f32[40,1,128]{2,1,0:T(1,128)} %bitcast.44, bf16[32000,2304]{1,0:T(8,128)(2,1)} %table_ref.7, bf16[320,2304]{1,0:T(8,128)(2,1)} %get-tuple-element.44.rest_0_, bf16[320,2304]{1,0:T(8,128)(2,1)} %copy-done.2, ...), custom_call_target="tpu_custom_call" | custom-call | flops 25600000000 | bytes 17694720 | tf_op jit(solution)/shard_map/gather_rows/pallas_call | solution.py:101
  74.6 21.8 %collective-permute-start.12 = (bf16[1280,2304]{1,0:T(8,128)(2,1)}, bf16[1280,2304]{1,0:T(8,128)(2,1)}, u32[]{:S(2)}, u32[]{:S(2)}) collective-permute-start(bf16[1280,2304]{1,0:T(8,128)(2,1)} %gather_rows.6.rest_0_), channel_id=1, source_target_pairs={{0,1},{1,0},{2,3},{3,2},{4,5},{5,4},{6,7},{7,6},{8,9},{9,8},{10,11... | collective-permute-start | bytes 17694728 | tf_op jit(solution)/shard_map/ppermute | solution.py:374
  96.4 2.3 slice_add_fusion.11
  98.7 1.7 broadcast_select_fusion.1
  100.7 1.8 pad_maximum_fusion
  102.5 1.3 collective-permute-start.8
  103.8 1.6 constant_dynamic-slice_fusion
  105.4 1.3 collective-permute-start.17
  106.6 9.7 %gather_rows.7 = bf16[1280,2304]{1,0:T(8,128)(2,1)} custom-call(s32[5120]{0:T(1024)} %bitcast.41, s32[40]{0:T(128)} %get-tuple-element.81.counts, f32[40,1,128]{2,1,0:T(1,128)} %bitcast.45, bf16[32000,2304]{1,0:T(8,128)(2,1)} %table_ref.7, bf16[1280,2304]{1,0:T(8,128)(2,1)} %gather_rows.6.rest_0_), custom_call_target="tpu_custom_call" | custom-call | flops 25600000000 | bytes 17694720 | tf_op jit(solution)/shard_map/gather_rows/pallas_call | solution.py:101
  116.3 4.8 %slice_add_fusion = (bf16[320,2304]{1,0:T(8,128)(2,1)}, bf16[320,2304]{1,0:T(8,128)(2,1)}) fusion(bf16[1280,2304]{1,0:T(8,128)(2,1)} %collective-permute-done.12, bf16[1280,2304]{1,0:T(8,128)(2,1)} %gather_rows.7), kind=kLoop, calls=%fused_computation.21 | loop fusion | flops 1474560 | bytes 8847360 | tf_op jit(solution)/shard_map/add | solution.py:464
  121.5 3.6 slice_add_fusion.6
  125.1 1.5 collective-permute-start.13
  128.8 1.0 copy.19.cols_ref
  131.2 3.0 multiply_sine_fusion
  134.2 5.1 %pmax.7 = s32[]{:T(128)} all-reduce(s32[]{:T(128)S(6)} %convert_element_type.29), channel_id=1, replica_groups=mesh['dp'=2,'tp'=8] {'dp'}, use_global_device_ids=true, to_apply=%region_5.6 | all-reduce | flops 1 | bytes 8 | tf_op jit(solution)/shard_map/pmax | solution.py:488
  140.0 1.3 conditional.1
  140.0 1.3 broadcast.217
  141.3 2.4 collective-permute-start.15
  143.8 1.4 slice_add_fusion.10
  145.4 1.5 collective-permute-done.13.refs_1_
  146.8 24.1 %collective-permute-start.18 = (bf16[4,1152,256]{2,1,0:T(8,128)(2,1)}, bf16[4,1152,256]{2,1,0:T(8,128)(2,1)}, u32[]{:S(2)}, u32[]{:S(2)}) collective-permute-start(bf16[4,1152,256]{2,1,0:T(8,128)(2,1)} %collective-permute-done.17.wq_far), channel_id=1, source_target_pairs={{0,1},{1,0},{2,3},{3,2},{4,5},{5,4},{6,7},{7,6},{8,9},{9,8},{10,11... | collective-permute-start | bytes 7077896 | tf_op jit(solution)/shard_map/ppermute | solution.py:374
  170.9 2.1 slice_add_fusion.5
  174.1 0.9 slice_add_fusion.4
  175.1 4.3 %collective-permute-start.16 = (bf16[160,2304]{1,0:T(8,128)(2,1)}, bf16[160,2304]{1,0:T(8,128)(2,1)}, u32[]{:S(2)}, u32[]{:S(2)}) collective-permute-start(bf16[160,2304]{1,0:T(8,128)(2,1)} %slice_add_fusion.4), channel_id=1, source_target_pairs={{0,2},{1,3},{2,0},{3,1},{4,6},{5,7},{6,4},{7,5},{8,10},{9,11},{10,... | collective-permute-start | bytes 2211848 | tf_op jit(solution)/shard_map/ppermute | solution.py:374
  179.4 4.1 %broadcast_select_fusion.base_hbm = bf16[640,2304]{1,0:T(8,128)(2,1)} fusion(bf16[640,2304]{1,0:T(8,128)(2,1)} %collective-permute-done.8, pred[]{:T(512)S(6)} %eq.54, bf16[320,2304]{1,0:T(8,128)(2,1)S(1)} %broadcast_select_fusion.1, bf16[320,2304]{1,0:T(8,128)(2,1)S(1)} %broadcast_select_fusion.6), kind=kLoop, calls=%fused_computation.18 | loop fusion | flops 7372800 | bytes 8847361 | tf_op jit(solution)/shard_map/jit(_where)/select_n | solution.py:395
  184.4 12.0 %pick_rows.2.base_hbm = bf16[1024,2304]{1,0:T(8,128)(2,1)} custom-call(s32[1]{0:T(128)} %bitcast.6.more, s32[1024,1]{1,0:T(8,128)} %copy.19.cols_ref, f32[1,2304]{1,0:T(1,128)} %broadcast_in_dim.89.gain_ref, bf16[640,2304]{1,0:T(8,128)(2,1)} %broadcast_select_fusion.base_hbm, bf16[384,2304]{1,0:T(8,128)(2,1)} %get-tuple-element.94.extra_hbm, ...), custom_call_target="tpu_custom_call" | custom-call | flops 4529848320 | bytes 16000000 | tf_op jit(solution)/shard_map/pick_rows/pallas_call | solution.py:202
  196.4 11.8 %pick_rows.3 = (bf16[1024,2304]{1,0:T(8,128)(2,1)}, bf16[1024,2304]{1,0:T(8,128)(2,1)}) custom-call(s32[1]{0:T(128)} %bitcast.6.more, s32[1024,1]{1,0:T(8,128)} %copy.19.cols_ref, f32[1,2304]{1,0:T(1,128)} %broadcast_in_dim.89.gain_ref, bf16[1024,2304]{1,0:T(8,128)(2,1)} %pick_rows.2.base_hbm, bf16[384,2304]{1,0:T(8,128)(2,1)} %get-tuple-element.94.extra_hbm, ...), custom_call_target="tpu_custom_call" | custom-call | flops 1509949440 | bytes 16000000 | tf_op jit(solution)/shard_map/pick_rows/pallas_call | solution.py:202
  208.2 139.9 %project_heads.1 = (bf16[8192,256]{1,0:T(8,128)(2,1)}, bf16[2,8192,256]{2,1,0:T(8,128)(2,1)}) custom-call(bf16[1024,2304]{1,0:T(8,128)(2,1)} %get-tuple-element.54.normed_hbm, f32[1024,128]{1,0:T(8,128)} %get-tuple-element.84.cos_ref, f32[1024,128]{1,0:T(8,128)} %get-tuple-element.83.sin_ref, bf16[8,1152,256]{2,1,0:T(8,128)(2,1)} %bitcast.33, ...), custom_call_target="tpu_custom_call" | custom-call | flops 19327352832 | bytes 40000000 | tf_op jit(solution)/shard_map/project_heads/pallas_call | solution.py:345
  348.2 6.6 %slice_bitcast_fusion = (bf16[8192,1,256]{2,0,1:T(8,128)(2,1)}, bf16[8192,1,256]{2,0,1:T(8,128)(2,1)}) fusion(bf16[2,8192,256]{2,1,0:T(8,128)(2,1)} %get-tuple-element.56), kind=kLoop, calls=%fused_computation.13 | loop fusion | bytes 16777216 | tf_op jit(solution)/shard_map/broadcast_in_dim;squeeze | solution.py:499
  355.4 2.0 copy.28
  (96 shorter events, 10.5 us)
Async XLA Ops:
  7.2 7.8 %copy-start.13 = (s32[8192]{0:T(1024)S(1)}, s32[8192]{0:T(1024)}, u32[]{:S(2)}) copy-start(s32[8192]{0:T(1024)} %param.9) | copy-start | bytes 98308
  7.2 57.3 %all-gather.3.cloned.1.call-start = ((), (), s32[]{:S(2)}) async-start(), calls=%async_computation.2 | async-start | bytes 5308416 | tf_op jit(solution)/shard_map/all_gather | solution.py:403
  10.3 24.8 %collective-permute-start.2 = (bf16[320,2304]{1,0:T(8,128)(2,1)}, bf16[320,2304]{1,0:T(8,128)(2,1)S(1)}, u32[]{:S(2)}, u32[]{:S(2)}) collective-permute-start(bf16[320,2304]{1,0:T(8,128)(2,1)} %get-tuple-element.61), channel_id=1, source_target_pairs={{0,2},{8,10}} | collective-permute-start | bytes 4423688 | tf_op jit(solution)/shard_map/ppermute | solution.py:377
  11.1 25.2 %collective-permute-start.5 = (bf16[320,2304]{1,0:T(8,128)(2,1)S(1)}, bf16[320,2304]{1,0:T(8,128)(2,1)}, u32[]{:S(2)}, u32[]{:S(2)}) collective-permute-start(bf16[320,2304]{1,0:T(8,128)(2,1)S(1)} %get-tuple-element.62), channel_id=1, source_target_pairs={{0,4},{8,12}} | collective-permute-start | bytes 4423688 | tf_op jit(solution)/shard_map/ppermute | solution.py:377
  15.0 0.7 copy-start.12
  15.7 0.6 copy-start.15
  16.6 17.3 %copy-start.10 = (s32[8,1024]{1,0:T(8,128)}, s32[8,1024]{1,0:T(8,128)S(1)}, u32[]{:S(2)}) copy-start(s32[8,1024]{1,0:T(8,128)S(1)} %fusion.3) | copy-start | bytes 98308
  33.9 23.1 %collective-permute-start = (bf16[1280,2304]{1,0:T(8,128)(2,1)}, bf16[1280,2304]{1,0:T(8,128)(2,1)}, u32[]{:S(2)}, u32[]{:S(2)}) collective-permute-start(bf16[1280,2304]{1,0:T(8,128)(2,1)} %gather_rows.4.rest_0_), channel_id=1, source_target_pairs={{0,1},{1,0},{2,3},{3,2},{4,5},{5,4},{6,7},{7,6},{8,9},{9,8},{10,11... | collective-permute-start | bytes 17694728 | tf_op jit(solution)/shard_map/ppermute | solution.py:374
  35.2 1.1 copy-start.9
  38.4 13.4 %collective-permute-start.6 = (bf16[320,2304]{1,0:T(8,128)(2,1)S(1)}, bf16[320,2304]{1,0:T(8,128)(2,1)}, u32[]{:S(2)}, u32[]{:S(2)}) collective-permute-start(bf16[320,2304]{1,0:T(8,128)(2,1)S(1)} %get-tuple-element.60), channel_id=1, source_target_pairs={{4,6},{12,14}} | collective-permute-start | bytes 4423688 | tf_op jit(solution)/shard_map/ppermute | solution.py:377
  40.2 14.8 %collective-permute-start.3 = (bf16[320,2304]{1,0:T(8,128)(2,1)S(1)}, bf16[320,2304]{1,0:T(8,128)(2,1)}, u32[]{:S(2)}, u32[]{:S(2)}) collective-permute-start(bf16[320,2304]{1,0:T(8,128)(2,1)S(1)} %get-tuple-element.59), channel_id=1, source_target_pairs={{2,6},{10,14}} | collective-permute-start | bytes 4423688 | tf_op jit(solution)/shard_map/ppermute | solution.py:377
  51.7 5.2 %copy-start = (bf16[1280,2304]{1,0:T(8,128)(2,1)S(1)}, bf16[1280,2304]{1,0:T(8,128)(2,1)}, u32[]{:S(2)}) copy-start(bf16[1280,2304]{1,0:T(8,128)(2,1)} %gather_rows.5) | copy-start | bytes 17694724
  53.0 45.7 %collective-permute-start.7 = (bf16[320,2304]{1,0:T(8,128)(2,1)}, bf16[320,2304]{1,0:T(8,128)(2,1)}, u32[]{:S(2)}, u32[]{:S(2)}) collective-permute-start(bf16[320,2304]{1,0:T(8,128)(2,1)} %broadcast_select_fusion.3), channel_id=1, source_target_pairs={{6,2},{14,10}} | collective-permute-start | bytes 4423688 | tf_op jit(solution)/shard_map/ppermute | solution.py:377
  55.1 5.5 %copy-start.3 = (bf16[320,2304]{1,0:T(8,128)(2,1)}, bf16[320,2304]{1,0:T(8,128)(2,1)S(1)}, u32[]{:S(2)}) copy-start(bf16[320,2304]{1,0:T(8,128)(2,1)S(1)} %broadcast_select_fusion.4) | copy-start | bytes 4423684
  55.1 43.6 %collective-permute-start.4 = (bf16[320,2304]{1,0:T(8,128)(2,1)S(1)}, bf16[320,2304]{1,0:T(8,128)(2,1)}, u32[]{:S(2)}, u32[]{:S(2)}) collective-permute-start(bf16[320,2304]{1,0:T(8,128)(2,1)S(1)} %broadcast_select_fusion.4), channel_id=1, source_target_pairs={{6,4},{14,12}} | collective-permute-start | bytes 4423688 | tf_op jit(solution)/shard_map/ppermute | solution.py:377
  64.0 1.1 copy-start.2
  64.0 32.5 %collective-permute-start.1 = (bf16[320,2304]{1,0:T(8,128)(2,1)S(1)}, bf16[320,2304]{1,0:T(8,128)(2,1)}, u32[]{:S(2)}, u32[]{:S(2)}) collective-permute-start(bf16[320,2304]{1,0:T(8,128)(2,1)S(1)} %get-tuple-element.39.rest_1_), channel_id=1, source_target_pairs={{0,4},{1,5},{2,6},{3,7},{4,0},{5,1},{6,2},{7,3},{8,12},{9,13},{10,... | collective-permute-start | bytes 4423688 | tf_op jit(solution)/shard_map/ppermute | solution.py:374
  74.6 41.7 %collective-permute-start.12 = (bf16[1280,2304]{1,0:T(8,128)(2,1)}, bf16[1280,2304]{1,0:T(8,128)(2,1)}, u32[]{:S(2)}, u32[]{:S(2)}) collective-permute-start(bf16[1280,2304]{1,0:T(8,128)(2,1)} %gather_rows.6.rest_0_), channel_id=1, source_target_pairs={{0,1},{1,0},{2,3},{3,2},{4,5},{5,4},{6,7},{7,6},{8,9},{9,8},{10,11... | collective-permute-start | bytes 17694728 | tf_op jit(solution)/shard_map/ppermute | solution.py:374
  96.4 44.9 %collective-permute-start.9 = (bf16[320,2304]{1,0:T(8,128)(2,1)}, bf16[320,2304]{1,0:T(8,128)(2,1)}, u32[]{:S(2)}, u32[]{:S(2)}) collective-permute-start(bf16[320,2304]{1,0:T(8,128)(2,1)} %get-tuple-element.44.rest_0_), channel_id=1, source_target_pairs={{0,2},{1,3},{2,0},{3,1},{4,6},{5,7},{6,4},{7,5},{8,10},{9,11},{10,... | collective-permute-start | bytes 4423688 | tf_op jit(solution)/shard_map/ppermute | solution.py:374
  98.7 1.8 copy-start.4
  98.7 5.1 %slice-start = ((s8[4718592]{0:T(1024)(128)(4,1)}), s8[4194304]{0:T(1024)(128)(4,1)S(1)}, s32[]{:S(2)}) async-start(s8[4718592]{0:T(1024)(128)(4,1)} %bitcast.34), calls=%async_computation.3 | async-start | bytes 8388608
  100.5 3.3 slice-start.1
  102.5 72.6 %collective-permute-start.8 = (bf16[640,2304]{1,0:T(8,128)(2,1)}, bf16[640,2304]{1,0:T(8,128)(2,1)}, u32[]{:S(2)}, u32[]{:S(2)}) collective-permute-start(bf16[640,2304]{1,0:T(8,128)(2,1)} %pad_maximum_fusion), channel_id=1, source_target_pairs={{0,1},{2,3},{4,5},{6,7},{8,9},{10,11},{12,13},{14,15}} | collective-permute-start | bytes 8847368 | tf_op jit(solution)/shard_map/ppermute | solution.py:394
  105.4 39.8 %collective-permute-start.17 = (bf16[4,1152,256]{2,1,0:T(8,128)(2,1)}, bf16[4,1152,256]{2,1,0:T(8,128)(2,1)}, u32[]{:S(2)}, u32[]{:S(2)}) collective-permute-start(bf16[4,1152,256]{2,1,0:T(8,128)(2,1)} %constant_dynamic-slice_fusion), channel_id=1, source_target_pairs={{0,8},{8,0},{1,9},{9,1},{2,10},{10,2},{3,11},{11,3},{4,12},{12,4},... | collective-permute-start | bytes 7077896 | tf_op jit(solution)/shard_map/ppermute | solution.py:404
  116.3 5.2 %copy-start.1 = (bf16[1280,2304]{1,0:T(8,128)(2,1)S(1)}, bf16[1280,2304]{1,0:T(8,128)(2,1)}, u32[]{:S(2)}) copy-start(bf16[1280,2304]{1,0:T(8,128)(2,1)} %gather_rows.7) | copy-start | bytes 17694724
  121.5 5.1 %copy-start.11 = (s32[8,1024]{1,0:T(8,128)S(1)}, s32[8,1024]{1,0:T(8,128)}, u32[]{:S(2)}) copy-start(s32[8,1024]{1,0:T(8,128)} %copy-done.10) | copy-start | bytes 98308
  121.5 5.1 %copy-start.16 = (pred[8,1024]{1,0:T(8,128)(4,1)S(1)}, pred[8,1024]{1,0:T(8,128)(4,1)}, u32[]{:S(2)}) copy-start(pred[8,1024]{1,0:T(8,128)(4,1)} %copy-done.15) | copy-start | bytes 24580
  121.5 5.9 %copy-start.18 = (s32[8]{0:T(128)S(1)}, s32[8]{0:T(128)}, u32[]{:S(2)}) copy-start(s32[8]{0:T(128)} %get-tuple-element.57) | copy-start | bytes 100
  121.5 8.4 %copy-start.17 = (f32[2304]{0:T(1024)S(1)}, f32[2304]{0:T(1024)}, u32[]{:S(2)}) copy-start(f32[2304]{0:T(1024)} %param.12) | copy-start | bytes 27652
  121.5 18.5 %copy-start.14 = (s32[8192]{0:T(1024)S(1)}, s32[8192]{0:T(1024)}, u32[]{:S(2)}) copy-start(s32[8192]{0:T(1024)} %param.9) | copy-start | bytes 98308
  125.1 21.7 %collective-permute-start.13 = (bf16[320,2304]{1,0:T(8,128)(2,1)}, bf16[320,2304]{1,0:T(8,128)(2,1)}, u32[]{:S(2)}, u32[]{:S(2)}) collective-permute-start(bf16[320,2304]{1,0:T(8,128)(2,1)} %get-tuple-element.48), channel_id=1, source_target_pairs={{0,2},{1,3},{2,0},{3,1},{4,6},{5,7},{6,4},{7,5},{8,10},{9,11},{10,... | collective-permute-start | bytes 4423688 | tf_op jit(solution)/shard_map/ppermute | solution.py:374
  134.2 50.1 %collective-permute-start.11 = (bf16[160,2304]{1,0:T(8,128)(2,1)}, bf16[160,2304]{1,0:T(8,128)(2,1)}, u32[]{:S(2)}, u32[]{:S(2)}) collective-permute-start(bf16[160,2304]{1,0:T(8,128)(2,1)} %slice_add_fusion.11), channel_id=1, source_target_pairs={{0,2},{1,3},{2,0},{3,1},{4,6},{5,7},{6,4},{7,5},{8,10},{9,11},{10,... | collective-permute-start | bytes 2211848 | tf_op jit(solution)/shard_map/ppermute | solution.py:374
  141.3 29.6 %copy-start.8 = (bf16[160,2304]{1,0:T(8,128)(2,1)S(1)}, bf16[160,2304]{1,0:T(8,128)(2,1)}, u32[]{:S(2)}) copy-start(bf16[160,2304]{1,0:T(8,128)(2,1)} %get-tuple-element.49) | copy-start | bytes 2211844
  141.3 32.8 %copy-start.7 = (bf16[160,2304]{1,0:T(8,128)(2,1)S(1)}, bf16[160,2304]{1,0:T(8,128)(2,1)}, u32[]{:S(2)}) copy-start(bf16[160,2304]{1,0:T(8,128)(2,1)} %get-tuple-element.52) | copy-start | bytes 2211844
  141.3 31.7 %collective-permute-start.15 = (bf16[320,2304]{1,0:T(8,128)(2,1)}, bf16[320,2304]{1,0:T(8,128)(2,1)S(1)}, u32[]{:S(2)}, u32[]{:S(2)}) collective-permute-start(bf16[320,2304]{1,0:T(8,128)(2,1)} %get-tuple-element.51), channel_id=1, source_target_pairs={{0,4},{1,5},{2,6},{3,7},{4,0},{5,1},{6,2},{7,3},{8,12},{9,13},{10,... | collective-permute-start | bytes 4423688 | tf_op jit(solution)/shard_map/ppermute | solution.py:374
  145.2 38.3 %collective-permute-start.10 = (bf16[160,2304]{1,0:T(8,128)(2,1)S(1)}, bf16[160,2304]{1,0:T(8,128)(2,1)S(1)}, u32[]{:S(2)}, u32[]{:S(2)}) collective-permute-start(bf16[160,2304]{1,0:T(8,128)(2,1)S(1)} %slice_add_fusion.10), channel_id=1, source_target_pairs={{0,4},{1,5},{2,6},{3,7},{4,0},{5,1},{6,2},{7,3},{8,12},{9,13},{10,... | collective-permute-start | bytes 2211848 | tf_op jit(solution)/shard_map/ppermute | solution.py:374
  146.8 61.4 %collective-permute-start.18 = (bf16[4,1152,256]{2,1,0:T(8,128)(2,1)}, bf16[4,1152,256]{2,1,0:T(8,128)(2,1)}, u32[]{:S(2)}, u32[]{:S(2)}) collective-permute-start(bf16[4,1152,256]{2,1,0:T(8,128)(2,1)} %collective-permute-done.17.wq_far), channel_id=1, source_target_pairs={{0,1},{1,0},{2,3},{3,2},{4,5},{5,4},{6,7},{7,6},{8,9},{9,8},{10,11... | collective-permute-start | bytes 7077896 | tf_op jit(solution)/shard_map/ppermute | solution.py:374
  173.0 1.1 copy-start.6
  173.0 23.4 %collective-permute-start.14 = (bf16[160,2304]{1,0:T(8,128)(2,1)}, bf16[160,2304]{1,0:T(8,128)(2,1)}, u32[]{:S(2)}, u32[]{:S(2)}) collective-permute-start(bf16[160,2304]{1,0:T(8,128)(2,1)} %slice_add_fusion.5), channel_id=1, source_target_pairs={{0,4},{1,5},{2,6},{3,7},{4,0},{5,1},{6,2},{7,3},{8,12},{9,13},{10,... | collective-permute-start | bytes 2211848 | tf_op jit(solution)/shard_map/ppermute | solution.py:374
  175.1 21.4 %collective-permute-start.16 = (bf16[160,2304]{1,0:T(8,128)(2,1)}, bf16[160,2304]{1,0:T(8,128)(2,1)}, u32[]{:S(2)}, u32[]{:S(2)}) collective-permute-start(bf16[160,2304]{1,0:T(8,128)(2,1)} %slice_add_fusion.4), channel_id=1, source_target_pairs={{0,2},{1,3},{2,0},{3,1},{4,6},{5,7},{6,4},{7,5},{8,10},{9,11},{10,... | collective-permute-start | bytes 2211848 | tf_op jit(solution)/shard_map/ppermute | solution.py:374
  183.5 0.9 copy-start.19
  348.2 7.2 %copy-start.5 = (bf16[8192,256]{1,0:T(8,128)(2,1)S(1)}, bf16[8192,256]{1,0:T(8,128)(2,1)}, u32[]{:S(2)}) copy-start(bf16[8192,256]{1,0:T(8,128)(2,1)} %get-tuple-element.55) | copy-start | bytes 12582916
Sparse Core Ops, SparseCore 0:
  15.1 40.4 all-gather.2
where the time goes:
time: 366 us; the launch traced here: 364 us
  Pallas kernels  202 us (55%)
  starting transfers between devices  69.4 us (19%)
  other arithmetic  45.1 us (12%)
  local copies, waits for them, and re-layouts  23.2 us (6%)
  between operations  15.9 us (4%)
  blocking collectives  5.09 us (1%)
    pallas_call x1, Pallas kernels, project_heads(): pl.pallas_call(functools.partial(heads_kernel, rows), out_shape=(jax.Shap...  140 us
    ppermute x11, starting transfers between devices, exchange(): return lax.ppermute(rows, 'tp', [(i, i ^ bit) for i in range(group_size)])  56.8 us
    pallas_call x4, Pallas kernels, gather_rows(): pl.pallas_call(functools.partial(gather_kernel, base, tiles, width), grid...  38.6 us
    pallas_call x2, Pallas kernels, pick_rows(): pl.pallas_call(functools.partial(rows_kernel, len(pieces), head_rows, fir...  23.8 us
    add x4, other arithmetic, local_body(): both = lax.optimization_barrier([mine[span] + got[span] for span in spans])  15.4 us
    ppermute x6, starting transfers between devices, pass_head(): got = lax.ppermute(values, 'tp', pairs)  10 us
  transfers between devices with their start and end apart: 20, of which 1 were waited for; matrix products, arithmetic and copies ran while one was open for 15% of the time, Pallas kernels for 17%

commit v1 on v0

--- a/solution.py
+++ b/solution.py
@@ -11,11 +11,10 @@
 EPSILON = 1e-6
 ROPE_BASE = 10000.0
 TILE = 128
-SLOTS = 6
 CHUNKS = 2
-HEAD_ROWS = 640
+HEAD_ROWS = 512
 TAIL_ROWS = 640
-SEND_ROWS = 512
+SEND_ROWS = 256
 CHIPS = 4
 MESH_IDS = pl.DeviceIdType.MESH
 
@@ -65,16 +64,14 @@
     @pl.when(step == 0)
     def _():
         pairs[...] = jnp.zeros_like(pairs)
-
-        @pl.loop(0, min(SLOTS - 1, tiles))
-        def _(tile):
-            start(tile, tile)
-
-    slot = lax.rem(step, SLOTS)
-
-    @pl.when(step + SLOTS - 1 < tiles)
+        start(0, 0)
+        start(1, 1)
+
+    slot = lax.rem(step, 3)
+
+    @pl.when(step + 2 < tiles)
     def _():
-        start(step + SLOTS - 1, lax.rem(step + SLOTS - 1, SLOTS))
+        start(step + 2, lax.rem(step + 2, 3))
 
     wait(step, slot)
     lanes = lax.broadcasted_iota(jnp.int32, (TILE, 2 * TILE), 1).astype(jnp.float32)
@@ -96,7 +93,7 @@
         grid=(tiles,),
         in_specs=[pl.BlockSpec(cols.shape, lambda i, *_: (0, 0, 0)), anywhere] + [anywhere] * len(after),
         out_specs=pl.BlockSpec((TILE, width), lambda i, *_: (i, 0)),
-        scratch_shapes=[pltpu.VMEM((SLOTS, TILE // 8, 16, width), jnp.bfloat16), pltpu.SemaphoreType.DMA((SLOTS,))],
+        scratch_shapes=[pltpu.VMEM((3, TILE // 8, 16, width), jnp.bfloat16), pltpu.SemaphoreType.DMA((3,))],
     )
     return pl.pallas_call(
         functools.partial(gather_kernel, base, tiles, width),
@@ -229,7 +226,7 @@
     sources = ((normed_hbm, normed), (wk_hbm, wk), (wv_hbm, wv), (wq_mine, wq.at[:, own_depth, :]),
                (wq_far, wq.at[pl.ds(core * CHIPS, CHIPS), far_depth, :]), (wq_near, wq.at[pl.ds((1 - core) * CHIPS, CHIPS), far_depth, :]))
     loads = [pltpu.make_async_copy(src, dst, w_sem.at[n]) for n, (src, dst) in enumerate(sources)]
-    for load in loads[:2]:
+    for load in loads:
         load.start()
 
     barrier = pltpu.get_barrier_semaphore()
@@ -237,10 +234,8 @@
         pl.semaphore_signal(barrier, inc=1, device_id=(group, lax.rem(me + step, 2 * CHIPS)), device_id_type=MESH_IDS)
 
     pl.semaphore_wait(barrier, 2 * CHIPS - 1)
-    for load in loads[:2]:
+    for load in loads:
         load.wait()
-    for load in loads[2:]:
-        load.start()
 
     def block(source, tile):
         return pl.ds(pl.multiple_of(source * rows + tile * SEND_ROWS, SEND_ROWS), SEND_ROWS)
@@ -274,16 +269,8 @@
             def linear(weight):
                 return jnp.dot(lhs, weight, preferred_element_type=jnp.float32).astype(jnp.bfloat16)
 
-            def arrived(weights):
-                @pl.when(turn + part == 0)
-                def _():
-                    for load in weights:
-                        load.wait()
-
             kv_stage[0, there, span, :] = rotated(linear(wk[:, columns]).astype(jnp.float32), span, 1.0)
-            arrived(loads[2:3])
             kv_stage[1, there, span, :] = linear(wv[:, columns])
-            arrived(loads[3:])
             for side in range(2):
                 q_stage[2 * there + side, span, :] = rotated(linear(wq[2 * there + side]).astype(jnp.float32), span, HEAD_DIM ** -0.5)
 

time: 366 us -> 347 us (0.948)
  the two profiles are of different devices: /device:TPU:3 before, /device:TPU:0 now
where the time goes in v1:
time: 347 us; the launch traced here: 341 us
  Pallas kernels  168 us (48%)
  other arithmetic  41.1 us (12%)
  waiting for transfers between devices  41 us (12%)
  starting transfers between devices  37.5 us (11%)
  local copies, waits for them, and re-layouts  22.6 us (7%)
  between operations  15.9 us (5%)
  blocking collectives  13.1 us (4%)
    pallas_call x1, Pallas kernels, project_heads(): pl.pallas_call(functools.partial(heads_kernel, rows), out_shape=(jax.Shap...  95.3 us
    pallas_call x4, Pallas kernels, gather_rows(): pl.pallas_call(functools.partial(gather_kernel, base, tiles, width), grid...  49 us
    ppermute x11, waiting for transfers between devices, exchange(): return lax.ppermute(rows, 'tp', [(i, i ^ bit) for i in range(group_size)])  37.6 us
    pallas_call x2, Pallas kernels, pick_rows(): pl.pallas_call(functools.partial(rows_kernel, len(pieces), head_rows, fir...  23.4 us
    ppermute x11, starting transfers between devices, exchange(): return lax.ppermute(rows, 'tp', [(i, i ^ bit) for i in range(group_size)])  22.3 us
    add x4, other arithmetic, local_body(): both = lax.optimization_barrier([mine[span] + got[span] for span in spans])  15.4 us
    pmax x1, blocking collectives, local_body(): more = lax.pmax(over, 'dp')  13.1 us
    ppermute x6, starting transfers between devices, pass_head(): got = lax.ppermute(values, 'tp', pairs)  9.23 us
  transfers between devices with their start and end apart: 20, of which 5 were waited for; matrix products, arithmetic and copies ran while one was open for 15% of the time, Pallas kernels for 21%

profile of v1, /device:TPU:0, one launch (start us, length us, event | category | flops | bytes accessed | tf_op | source)
XLA Modules:
  0.0 340.6 jit_solution(3012883952315498898)
XLA Ops:
  7.2 1.9 constant_dynamic-slice_fusion.1
  10.9 3.0 select_reduce_fusion.1
  14.6 1.4 fusion.9
  15.9 2.6 select_reduce_fusion.2
  18.5 12.7 %gather_rows.4.rest_0_ = bf16[1280,2304]{1,0:T(8,128)(2,1)} custom-call(s32[5120]{0:T(1024)} %bitcast.38, s32[40]{0:T(128)} %get-tuple-element.81.counts, f32[40,1,128]{2,1,0:T(1,128)} %bitcast.42, bf16[32000,2304]{1,0:T(8,128)(2,1)} %table_ref.7), custom_call_target="tpu_custom_call" | custom-call | flops 25600000000 | bytes 17694720 | tf_op jit(solution)/shard_map/gather_rows/pallas_call | solution.py:98
  31.3 1.8 fusion.13
  33.1 1.9 collective-permute-start.2
  35.0 2.3 collective-permute-start.5
  37.3 12.7 %gather_rows.5 = bf16[1280,2304]{1,0:T(8,128)(2,1)} custom-call(s32[5120]{0:T(1024)} %bitcast.39, s32[40]{0:T(128)} %get-tuple-element.81.counts, f32[40,1,128]{2,1,0:T(1,128)} %bitcast.43, bf16[32000,2304]{1,0:T(8,128)(2,1)} %table_ref.7, bf16[1280,2304]{1,0:T(8,128)(2,1)} %gather_rows.4.rest_0_), custom_call_target="tpu_custom_call" | custom-call | flops 25600000000 | bytes 17694720 | tf_op jit(solution)/shard_map/gather_rows/pallas_call | solution.py:98
  52.1 1.0 copy.19.cols_ref
  53.2 3.4 collective-permute-done.2
  56.5 1.0 copy-done.13
  57.5 2.9 broadcast_select_fusion.2
  60.4 1.7 collective-permute-start.6
  62.1 1.7 collective-permute-start.3
  63.8 3.6 %slice_add_fusion.12 = (bf16[160,2304]{1,0:T(8,128)(2,1)}, bf16[160,2304]{1,0:T(8,128)(2,1)}, bf16[160,2304]{1,0:T(8,128)(2,1)}, bf16[160,2304]{1,0:T(8,128)(2,1)}) fusion(bf16[1280,2304]{1,0:T(8,128)(2,1)} %collective-permute-done, bf16[1280,2304]{1,0:T(8,128)(2,1)S(1)} %copy-done), kind=kLoop, calls=%fused_computation.45 | loop fusion | flops 1474560 | bytes 8847360 | tf_op jit(solution)/shard_map/add | solution.py:451
  67.4 3.4 slice_add_fusion.2
  70.8 2.5 collective-permute-start.1
  73.4 11.9 %gather_rows.6.rest_0_ = bf16[1280,2304]{1,0:T(8,128)(2,1)} custom-call(s32[5120]{0:T(1024)} %bitcast.40, s32[40]{0:T(128)} %get-tuple-element.81.counts, f32[40,1,128]{2,1,0:T(1,128)} %bitcast.44, bf16[32000,2304]{1,0:T(8,128)(2,1)} %table_ref.7, bf16[320,2304]{1,0:T(8,128)(2,1)} %get-tuple-element.44.rest_0_, bf16[320,2304]{1,0:T(8,128)(2,1)} %copy-done.2, ...), custom_call_target="tpu_custom_call" | custom-call | flops 25600000000 | bytes 17694720 | tf_op jit(solution)/shard_map/gather_rows/pallas_call | solution.py:98
  85.4 1.6 broadcast_select_fusion.3
  89.5 3.1 multiply_sine_fusion
  92.5 4.7 %collective-permute-start.9 = (bf16[320,2304]{1,0:T(8,128)(2,1)}, bf16[320,2304]{1,0:T(8,128)(2,1)}, u32[]{:S(2)}, u32[]{:S(2)}) collective-permute-start(bf16[320,2304]{1,0:T(8,128)(2,1)} %get-tuple-element.44.rest_0_), channel_id=1, source_target_pairs={{0,2},{1,3},{2,0},{3,1},{4,6},{5,7},{6,4},{7,5},{8,10},{9,11},{10,... | collective-permute-start | bytes 4423688 | tf_op jit(solution)/shard_map/ppermute | solution.py:361
  97.2 1.0 collective-permute-done.1.refs_4_
  98.2 2.1 slice_add_fusion.11
  100.3 1.0 copy-done.11
  101.4 1.6 constant_dynamic-slice_fusion
  103.0 3.3 collective-permute-start.17
  106.3 11.7 %gather_rows.7 = bf16[1280,2304]{1,0:T(8,128)(2,1)} custom-call(s32[5120]{0:T(1024)} %bitcast.41, s32[40]{0:T(128)} %get-tuple-element.81.counts, f32[40,1,128]{2,1,0:T(1,128)} %bitcast.45, bf16[32000,2304]{1,0:T(8,128)(2,1)} %table_ref.7, bf16[1280,2304]{1,0:T(8,128)(2,1)} %gather_rows.6.rest_0_), custom_call_target="tpu_custom_call" | custom-call | flops 25600000000 | bytes 17694720 | tf_op jit(solution)/shard_map/gather_rows/pallas_call | solution.py:98
  118.1 4.8 %slice_add_fusion = (bf16[320,2304]{1,0:T(8,128)(2,1)}, bf16[320,2304]{1,0:T(8,128)(2,1)}) fusion(bf16[1280,2304]{1,0:T(8,128)(2,1)} %collective-permute-done.12, bf16[1280,2304]{1,0:T(8,128)(2,1)} %gather_rows.7), kind=kLoop, calls=%fused_computation.21 | loop fusion | flops 1474560 | bytes 8847360 | tf_op jit(solution)/shard_map/add | solution.py:451
  123.2 3.6 %slice_add_fusion.6 = (bf16[160,2304]{1,0:T(8,128)(2,1)}, bf16[160,2304]{1,0:T(8,128)(2,1)}, bf16[160,2304]{1,0:T(8,128)(2,1)}, bf16[160,2304]{1,0:T(8,128)(2,1)}) fusion(bf16[1280,2304]{1,0:T(8,128)(2,1)} %collective-permute-done.12, bf16[1280,2304]{1,0:T(8,128)(2,1)S(1)} %copy-done.1), kind=kLoop, calls=%fused_computation.39 | loop fusion | flops 1474560 | bytes 8847360 | tf_op jit(solution)/shard_map/add | solution.py:451
  126.8 7.0 %collective-permute-start.13 = (bf16[320,2304]{1,0:T(8,128)(2,1)}, bf16[320,2304]{1,0:T(8,128)(2,1)}, u32[]{:S(2)}, u32[]{:S(2)}) collective-permute-start(bf16[320,2304]{1,0:T(8,128)(2,1)} %get-tuple-element.48), channel_id=1, source_target_pairs={{0,2},{1,3},{2,0},{3,1},{4,6},{5,7},{6,4},{7,5},{8,10},{9,11},{10,... | collective-permute-start | bytes 4423688 | tf_op jit(solution)/shard_map/ppermute | solution.py:361
  134.0 1.6 pad_maximum_fusion
  135.6 2.7 collective-permute-start.8
  138.9 13.1 %pmax.7 = s32[]{:T(128)} all-reduce(s32[]{:T(128)S(6)} %convert_element_type.29), channel_id=1, replica_groups=mesh['dp'=2,'tp'=8] {'dp'}, use_global_device_ids=true, to_apply=%region_5.6 | all-reduce | flops 1 | bytes 8 | tf_op jit(solution)/shard_map/pmax | solution.py:475
  152.6 1.4 conditional.1
  152.6 1.3 broadcast.217
  154.0 6.9 %collective-permute-start.15 = (bf16[320,2304]{1,0:T(8,128)(2,1)}, bf16[320,2304]{1,0:T(8,128)(2,1)S(1)}, u32[]{:S(2)}, u32[]{:S(2)}) collective-permute-start(bf16[320,2304]{1,0:T(8,128)(2,1)} %get-tuple-element.51), channel_id=1, source_target_pairs={{0,4},{1,5},{2,6},{3,7},{4,0},{5,1},{6,2},{7,3},{8,12},{9,13},{10,... | collective-permute-start | bytes 4423688 | tf_op jit(solution)/shard_map/ppermute | solution.py:361
  160.9 1.2 slice_add_fusion.10
  162.2 4.7 %collective-permute-done.13.refs_1_ = bf16[320,2304]{1,0:T(8,128)(2,1)} collective-permute-done((bf16[320,2304]{1,0:T(8,128)(2,1)}, bf16[320,2304]{1,0:T(8,128)(2,1)}, u32[]{:S(2)}, u32[]{:S(2)}) %collective-permute-start.13) | collective-permute-done | bytes 1474592 | tf_op jit(solution)/shard_map/ppermute | solution.py:361
  167.0 2.1 slice_add_fusion.5
  169.1 25.2 %collective-permute-done.15.refs_4_ = bf16[320,2304]{1,0:T(8,128)(2,1)S(1)} collective-permute-done((bf16[320,2304]{1,0:T(8,128)(2,1)}, bf16[320,2304]{1,0:T(8,128)(2,1)S(1)}, u32[]{:S(2)}, u32[]{:S(2)}) %collective-permute-start.15) | collective-permute-done | bytes 1474592 | tf_op jit(solution)/shard_map/ppermute | solution.py:361
  196.3 1.9 broadcast_select_fusion.base_hbm
  198.2 6.7 %collective-permute-done.10.refs_2_ = bf16[160,2304]{1,0:T(8,128)(2,1)S(1)} collective-permute-done((bf16[160,2304]{1,0:T(8,128)(2,1)S(1)}, bf16[160,2304]{1,0:T(8,128)(2,1)S(1)}, u32[]{:S(2)}, u32[]{:S(2)}) %collective-permute-start.10) | collective-permute-done | bytes 737312 | tf_op jit(solution)/shard_map/ppermute | solution.py:361
  205.8 11.6 %pick_rows.2.base_hbm = bf16[1024,2304]{1,0:T(8,128)(2,1)} custom-call(s32[1]{0:T(128)} %bitcast.6.more, s32[1024,1]{1,0:T(8,128)} %copy.19.cols_ref, f32[1,2304]{1,0:T(1,128)} %broadcast_in_dim.89.gain_ref, bf16[512,2304]{1,0:T(8,128)(2,1)} %broadcast_select_fusion.base_hbm, bf16[384,2304]{1,0:T(8,128)(2,1)} %get-tuple-element.94.extra_hbm, ...), custom_call_target="tpu_custom_call" | custom-call | flops 3925868544 | bytes 16000000 | tf_op jit(solution)/shard_map/pick_rows/pallas_call | solution.py:199
  217.5 11.8 %pick_rows.3 = (bf16[1024,2304]{1,0:T(8,128)(2,1)}, bf16[1024,2304]{1,0:T(8,128)(2,1)}) custom-call(s32[1]{0:T(128)} %bitcast.6.more, s32[1024,1]{1,0:T(8,128)} %copy.19.cols_ref, f32[1,2304]{1,0:T(1,128)} %broadcast_in_dim.89.gain_ref, bf16[1024,2304]{1,0:T(8,128)(2,1)} %pick_rows.2.base_hbm, bf16[384,2304]{1,0:T(8,128)(2,1)} %get-tuple-element.94.extra_hbm, ...), custom_call_target="tpu_custom_call" | custom-call | flops 1509949440 | bytes 16000000 | tf_op jit(solution)/shard_map/pick_rows/pallas_call | solution.py:199
  229.2 95.3 %project_heads.1 = (bf16[8192,256]{1,0:T(8,128)(2,1)}, bf16[2,8192,256]{2,1,0:T(8,128)(2,1)}) custom-call(bf16[1024,2304]{1,0:T(8,128)(2,1)} %get-tuple-element.54.normed_hbm, f32[1024,128]{1,0:T(8,128)} %get-tuple-element.84.cos_ref, f32[1024,128]{1,0:T(8,128)} %get-tuple-element.83.sin_ref, bf16[8,1152,256]{2,1,0:T(8,128)(2,1)} %bitcast.33, ...), custom_call_target="tpu_custom_call" | custom-call | flops 19327352832 | bytes 40000000 | tf_op jit(solution)/shard_map/project_heads/pallas_call | solution.py:332
  324.5 6.6 %slice_bitcast_fusion = (bf16[8192,1,256]{2,0,1:T(8,128)(2,1)}, bf16[8192,1,256]{2,0,1:T(8,128)(2,1)}) fusion(bf16[2,8192,256]{2,1,0:T(8,128)(2,1)} %get-tuple-element.56), kind=kLoop, calls=%fused_computation.13 | loop fusion | bytes 16777216 | tf_op jit(solution)/shard_map/broadcast_in_dim;squeeze | solution.py:486
  331.7 2.0 copy.28
  (96 shorter events, 11.2 us)
Async XLA Ops:
  7.2 66.2 %all-gather.3.cloned.1.call-start = ((), (), s32[]{:S(2)}) async-start(), calls=%async_computation.2 | async-start | bytes 5308416 | tf_op jit(solution)/shard_map/all_gather | solution.py:390
  10.0 0.6 copy-start.17
  10.9 20.3 %copy-start.15 = (s32[8,1024]{1,0:T(8,128)}, s32[8,1024]{1,0:T(8,128)S(1)}, u32[]{:S(2)}) copy-start(s32[8,1024]{1,0:T(8,128)S(1)} %fusion.3) | copy-start | bytes 98308
  31.2 32.6 %collective-permute-start = (bf16[1280,2304]{1,0:T(8,128)(2,1)}, bf16[1280,2304]{1,0:T(8,128)(2,1)}, u32[]{:S(2)}, u32[]{:S(2)}) collective-permute-start(bf16[1280,2304]{1,0:T(8,128)(2,1)} %gather_rows.4.rest_0_), channel_id=1, source_target_pairs={{0,1},{1,0},{2,3},{3,2},{4,5},{5,4},{6,7},{7,6},{8,9},{9,8},{10,11... | collective-permute-start | bytes 17694728 | tf_op jit(solution)/shard_map/ppermute | solution.py:361
  33.1 23.4 %collective-permute-start.2 = (bf16[256,2304]{1,0:T(8,128)(2,1)S(1)}, bf16[256,2304]{1,0:T(8,128)(2,1)S(1)}, u32[]{:S(2)}, u32[]{:S(2)}) collective-permute-start(bf16[256,2304]{1,0:T(8,128)(2,1)S(1)} %get-tuple-element.61), channel_id=1, source_target_pairs={{0,2},{8,10}} | collective-permute-start | bytes 3538952 | tf_op jit(solution)/shard_map/ppermute | solution.py:364
  35.0 22.5 %collective-permute-start.5 = (bf16[256,2304]{1,0:T(8,128)(2,1)S(1)}, bf16[256,2304]{1,0:T(8,128)(2,1)}, u32[]{:S(2)}, u32[]{:S(2)}) collective-permute-start(bf16[256,2304]{1,0:T(8,128)(2,1)S(1)} %get-tuple-element.62), channel_id=1, source_target_pairs={{0,4},{8,12}} | collective-permute-start | bytes 3538952 | tf_op jit(solution)/shard_map/ppermute | solution.py:364
  53.1 10.7 %copy-start = (bf16[1280,2304]{1,0:T(8,128)(2,1)S(1)}, bf16[1280,2304]{1,0:T(8,128)(2,1)}, u32[]{:S(2)}) copy-start(bf16[1280,2304]{1,0:T(8,128)(2,1)} %gather_rows.5) | copy-start | bytes 17694724
  56.5 1.0 copy-start.13
  60.4 7.1 %copy-start.3 = (bf16[256,2304]{1,0:T(8,128)(2,1)}, bf16[256,2304]{1,0:T(8,128)(2,1)S(1)}, u32[]{:S(2)}) copy-start(bf16[256,2304]{1,0:T(8,128)(2,1)S(1)} %get-tuple-element.59) | copy-start | bytes 3538948
  60.4 25.0 %collective-permute-start.6 = (bf16[256,2304]{1,0:T(8,128)(2,1)}, bf16[256,2304]{1,0:T(8,128)(2,1)}, u32[]{:S(2)}, u32[]{:S(2)}) collective-permute-start(bf16[256,2304]{1,0:T(8,128)(2,1)} %get-tuple-element.60), channel_id=1, source_target_pairs={{4,6},{12,14}} | collective-permute-start | bytes 3538952 | tf_op jit(solution)/shard_map/ppermute | solution.py:364
  62.1 25.8 %collective-permute-start.3 = (bf16[256,2304]{1,0:T(8,128)(2,1)S(1)}, bf16[256,2304]{1,0:T(8,128)(2,1)}, u32[]{:S(2)}, u32[]{:S(2)}) collective-permute-start(bf16[256,2304]{1,0:T(8,128)(2,1)S(1)} %get-tuple-element.59), channel_id=1, source_target_pairs={{2,6},{10,14}} | collective-permute-start | bytes 3538952 | tf_op jit(solution)/shard_map/ppermute | solution.py:364
  70.8 2.5 copy-start.2
  70.8 27.3 %collective-permute-start.1 = (bf16[320,2304]{1,0:T(8,128)(2,1)S(1)}, bf16[320,2304]{1,0:T(8,128)(2,1)}, u32[]{:S(2)}, u32[]{:S(2)}) collective-permute-start(bf16[320,2304]{1,0:T(8,128)(2,1)S(1)} %get-tuple-element.39.rest_1_), channel_id=1, source_target_pairs={{0,4},{1,5},{2,6},{3,7},{4,0},{5,1},{6,2},{7,3},{8,12},{9,13},{10,... | collective-permute-start | bytes 4423688 | tf_op jit(solution)/shard_map/ppermute | solution.py:361
  85.3 2.6 copy-start.4
  85.3 32.7 %collective-permute-start.12 = (bf16[1280,2304]{1,0:T(8,128)(2,1)}, bf16[1280,2304]{1,0:T(8,128)(2,1)}, u32[]{:S(2)}, u32[]{:S(2)}) collective-permute-start(bf16[1280,2304]{1,0:T(8,128)(2,1)} %gather_rows.6.rest_0_), channel_id=1, source_target_pairs={{0,1},{1,0},{2,3},{3,2},{4,5},{5,4},{6,7},{7,6},{8,9},{9,8},{10,11... | collective-permute-start | bytes 17694728 | tf_op jit(solution)/shard_map/ppermute | solution.py:361
  85.4 16.0 %slice-start = ((s8[4718592]{0:T(1024)(128)(4,1)}), s8[4194304]{0:T(1024)(128)(4,1)S(1)}, s32[]{:S(2)}) async-start(s8[4718592]{0:T(1024)(128)(4,1)} %bitcast.34), calls=%async_computation.3 | async-start | bytes 8388608
  86.9 11.2 %copy-start.10 = (bf16[160,2304]{1,0:T(8,128)(2,1)S(1)}, bf16[160,2304]{1,0:T(8,128)(2,1)}, u32[]{:S(2)}) copy-start(bf16[160,2304]{1,0:T(8,128)(2,1)} %get-tuple-element.38) | copy-start | bytes 2211844
  87.0 14.5 %slice-start.1 = ((s8[4718592]{0:T(1024)(128)(4,1)}), s8[524288]{0:T(1024)(128)(4,1)S(1)}, s32[]{:S(2)}) async-start(s8[4718592]{0:T(1024)(128)(4,1)} %bitcast.34), calls=%async_computation.4 | async-start | bytes 1048576
  87.0 13.3 %collective-permute-start.7 = (bf16[256,2304]{1,0:T(8,128)(2,1)S(1)}, bf16[256,2304]{1,0:T(8,128)(2,1)S(1)}, u32[]{:S(2)}, u32[]{:S(2)}) collective-permute-start(bf16[256,2304]{1,0:T(8,128)(2,1)S(1)} %broadcast_select_fusion.3), channel_id=1, source_target_pairs={{6,2},{14,10}} | collective-permute-start | bytes 3538952 | tf_op jit(solution)/shard_map/ppermute | solution.py:364
  88.0 12.3 %collective-permute-start.4 = (bf16[256,2304]{1,0:T(8,128)(2,1)S(1)}, bf16[256,2304]{1,0:T(8,128)(2,1)S(1)}, u32[]{:S(2)}, u32[]{:S(2)}) collective-permute-start(bf16[256,2304]{1,0:T(8,128)(2,1)S(1)} %broadcast_select_fusion.4), channel_id=1, source_target_pairs={{6,4},{14,12}} | collective-permute-start | bytes 3538952 | tf_op jit(solution)/shard_map/ppermute | solution.py:364
  92.5 61.5 %collective-permute-start.9 = (bf16[320,2304]{1,0:T(8,128)(2,1)}, bf16[320,2304]{1,0:T(8,128)(2,1)}, u32[]{:S(2)}, u32[]{:S(2)}) collective-permute-start(bf16[320,2304]{1,0:T(8,128)(2,1)} %get-tuple-element.44.rest_0_), channel_id=1, source_target_pairs={{0,2},{1,3},{2,0},{3,1},{4,6},{5,7},{6,4},{7,5},{8,10},{9,11},{10,... | collective-permute-start | bytes 4423688 | tf_op jit(solution)/shard_map/ppermute | solution.py:361
  100.3 1.0 copy-start.11
  103.0 59.1 %collective-permute-start.17 = (bf16[4,1152,256]{2,1,0:T(8,128)(2,1)}, bf16[4,1152,256]{2,1,0:T(8,128)(2,1)}, u32[]{:S(2)}, u32[]{:S(2)}) collective-permute-start(bf16[4,1152,256]{2,1,0:T(8,128)(2,1)} %constant_dynamic-slice_fusion), channel_id=1, source_target_pairs={{0,8},{8,0},{1,9},{9,1},{2,10},{10,2},{3,11},{11,3},{4,12},{12,4},... | collective-permute-start | bytes 7077896 | tf_op jit(solution)/shard_map/ppermute | solution.py:391
  118.0 5.2 %copy-start.1 = (bf16[1280,2304]{1,0:T(8,128)(2,1)S(1)}, bf16[1280,2304]{1,0:T(8,128)(2,1)}, u32[]{:S(2)}) copy-start(bf16[1280,2304]{1,0:T(8,128)(2,1)} %gather_rows.7) | copy-start | bytes 17694724
  123.2 10.6 %copy-start.12 = (bf16[256,2304]{1,0:T(8,128)(2,1)S(1)}, bf16[256,2304]{1,0:T(8,128)(2,1)}, u32[]{:S(2)}) copy-start(bf16[256,2304]{1,0:T(8,128)(2,1)} %copy-done.11) | copy-start | bytes 3538948
  126.8 40.2 %collective-permute-start.13 = (bf16[320,2304]{1,0:T(8,128)(2,1)}, bf16[320,2304]{1,0:T(8,128)(2,1)}, u32[]{:S(2)}, u32[]{:S(2)}) collective-permute-start(bf16[320,2304]{1,0:T(8,128)(2,1)} %get-tuple-element.48), channel_id=1, source_target_pairs={{0,2},{1,3},{2,0},{3,1},{4,6},{5,7},{6,4},{7,5},{8,10},{9,11},{10,... | collective-permute-start | bytes 4423688 | tf_op jit(solution)/shard_map/ppermute | solution.py:361
  134.0 4.3 %copy-start.19 = (f32[2304]{0:T(1024)S(1)}, f32[2304]{0:T(1024)}, u32[]{:S(2)}) copy-start(f32[2304]{0:T(1024)} %param.12) | copy-start | bytes 27652
  134.0 18.6 %copy-start.16 = (s32[8,1024]{1,0:T(8,128)S(1)}, s32[8,1024]{1,0:T(8,128)}, u32[]{:S(2)}) copy-start(s32[8,1024]{1,0:T(8,128)} %copy-done.15) | copy-start | bytes 98308
  134.0 18.6 %copy-start.18 = (s32[8192]{0:T(1024)S(1)}, s32[8192]{0:T(1024)}, u32[]{:S(2)}) copy-start(s32[8192]{0:T(1024)} %param.9) | copy-start | bytes 98308
  135.6 60.7 %collective-permute-start.8 = (bf16[512,2304]{1,0:T(8,128)(2,1)}, bf16[512,2304]{1,0:T(8,128)(2,1)}, u32[]{:S(2)}, u32[]{:S(2)}) collective-permute-start(bf16[512,2304]{1,0:T(8,128)(2,1)} %pad_maximum_fusion), channel_id=1, source_target_pairs={{0,1},{2,3},{4,5},{6,7},{8,9},{10,11},{12,13},{14,15}} | collective-permute-start | bytes 7077896 | tf_op jit(solution)/shard_map/ppermute | solution.py:381
  138.9 66.9 %collective-permute-start.11 = (bf16[160,2304]{1,0:T(8,128)(2,1)}, bf16[160,2304]{1,0:T(8,128)(2,1)}, u32[]{:S(2)}, u32[]{:S(2)}) collective-permute-start(bf16[160,2304]{1,0:T(8,128)(2,1)} %slice_add_fusion.11), channel_id=1, source_target_pairs={{0,2},{1,3},{2,0},{3,1},{4,6},{5,7},{6,4},{7,5},{8,10},{9,11},{10,... | collective-permute-start | bytes 2211848 | tf_op jit(solution)/shard_map/ppermute | solution.py:361
  152.6 8.3 %copy-start.7 = (bf16[160,2304]{1,0:T(8,128)(2,1)S(1)}, bf16[160,2304]{1,0:T(8,128)(2,1)}, u32[]{:S(2)}) copy-start(bf16[160,2304]{1,0:T(8,128)(2,1)} %get-tuple-element.45) | copy-start | bytes 2211844
  154.0 13.0 %copy-start.9 = (bf16[160,2304]{1,0:T(8,128)(2,1)S(1)}, bf16[160,2304]{1,0:T(8,128)(2,1)}, u32[]{:S(2)}) copy-start(bf16[160,2304]{1,0:T(8,128)(2,1)} %get-tuple-element.49) | copy-start | bytes 2211844
  154.0 41.4 %copy-start.8 = (bf16[160,2304]{1,0:T(8,128)(2,1)S(1)}, bf16[160,2304]{1,0:T(8,128)(2,1)}, u32[]{:S(2)}) copy-start(bf16[160,2304]{1,0:T(8,128)(2,1)} %get-tuple-element.52) | copy-start | bytes 2211844
  154.0 40.2 %collective-permute-start.15 = (bf16[320,2304]{1,0:T(8,128)(2,1)}, bf16[320,2304]{1,0:T(8,128)(2,1)S(1)}, u32[]{:S(2)}, u32[]{:S(2)}) collective-permute-start(bf16[320,2304]{1,0:T(8,128)(2,1)} %get-tuple-element.51), channel_id=1, source_target_pairs={{0,4},{1,5},{2,6},{3,7},{4,0},{5,1},{6,2},{7,3},{8,12},{9,13},{10,... | collective-permute-start | bytes 4423688 | tf_op jit(solution)/shard_map/ppermute | solution.py:361
  162.1 42.8 %collective-permute-start.10 = (bf16[160,2304]{1,0:T(8,128)(2,1)S(1)}, bf16[160,2304]{1,0:T(8,128)(2,1)S(1)}, u32[]{:S(2)}, u32[]{:S(2)}) collective-permute-start(bf16[160,2304]{1,0:T(8,128)(2,1)S(1)} %slice_add_fusion.10), channel_id=1, source_target_pairs={{0,4},{1,5},{2,6},{3,7},{4,0},{5,1},{6,2},{7,3},{8,12},{9,13},{10,... | collective-permute-start | bytes 2211848 | tf_op jit(solution)/shard_map/ppermute | solution.py:361
  167.0 62.2 %collective-permute-start.18 = (bf16[4,1152,256]{2,1,0:T(8,128)(2,1)}, bf16[4,1152,256]{2,1,0:T(8,128)(2,1)}, u32[]{:S(2)}, u32[]{:S(2)}) collective-permute-start(bf16[4,1152,256]{2,1,0:T(8,128)(2,1)} %collective-permute-done.17.wq_far), channel_id=1, source_target_pairs={{0,1},{1,0},{2,3},{3,2},{4,5},{5,4},{6,7},{7,6},{8,9},{9,8},{10,11... | collective-permute-start | bytes 7077896 | tf_op jit(solution)/shard_map/ppermute | solution.py:361
  194.2 1.1 copy-start.6
  194.2 23.2 %collective-permute-start.14 = (bf16[160,2304]{1,0:T(8,128)(2,1)}, bf16[160,2304]{1,0:T(8,128)(2,1)}, u32[]{:S(2)}, u32[]{:S(2)}) collective-permute-start(bf16[160,2304]{1,0:T(8,128)(2,1)} %slice_add_fusion.5), channel_id=1, source_target_pairs={{0,4},{1,5},{2,6},{3,7},{4,0},{5,1},{6,2},{7,3},{8,12},{9,13},{10,... | collective-permute-start | bytes 2211848 | tf_op jit(solution)/shard_map/ppermute | solution.py:361
  196.3 21.2 %collective-permute-start.16 = (bf16[160,2304]{1,0:T(8,128)(2,1)}, bf16[160,2304]{1,0:T(8,128)(2,1)}, u32[]{:S(2)}, u32[]{:S(2)}) collective-permute-start(bf16[160,2304]{1,0:T(8,128)(2,1)} %slice_add_fusion.4), channel_id=1, source_target_pairs={{0,2},{1,3},{2,0},{3,1},{4,6},{5,7},{6,4},{7,5},{8,10},{9,11},{10,... | collective-permute-start | bytes 2211848 | tf_op jit(solution)/shard_map/ppermute | solution.py:361
  204.9 0.9 copy-start.14
  324.5 7.2 %copy-start.5 = (bf16[8192,256]{1,0:T(8,128)(2,1)S(1)}, bf16[8192,256]{1,0:T(8,128)(2,1)}, u32[]{:S(2)}) copy-start(bf16[8192,256]{1,0:T(8,128)(2,1)} %get-tuple-element.55) | copy-start | bytes 12582916
Sparse Core Ops, SparseCore 0:
  9.8 38.0 all-gather.2
